TPU v7x, 128 devices: a whole 4x4x4 slice. The times are simulated.
128 devices in a mesh: group: 32 (over x, z, core), tensor: 4 (over y).
Axes of the slice: x: 4, y: 4, z: 4, core: 2. Of those that a mesh axis runs over, the one named last changes fastest.
Arguments:
- queries: bfloat16 [4096, 4096], P('group', 'tensor'), may hold values from -120 to 120
- keys: bfloat16 [4096, 512], P('group', 'tensor'), may hold values from -6 to 6
- values: bfloat16 [4096, 512], P('group', 'tensor'), may hold values from -6 to 6
- document_index: int32 [32, 128], P('group'), may hold values from 0 to 7, never falling along the last dimension, each value on 1 to 64 neighbouring positions
- out_proj: bfloat16 [4096, 4096], P('tensor', 'group'), may hold values from -0.25 to 0.25
- residual_in: bfloat16 [4096, 4096], P(('group', 'tensor')), may hold values from -60 to 60
- norm_gain: float32 [4096], replicated, may hold values from 0.1 to 1.9
- expert_ids: int32 [4096, 8], P(('group', 'tensor')), may hold values from 0 to 127, all different within a row; in each aligned block of 32 rows (0 to 31, 32 to 63, ...) at most 4 rows name the same one
- gate_weights: float32 [4096, 8], P(('group', 'tensor')), may hold values from 0.05 to 0.45
- w_gate_up: bfloat16 [128, 4096, 1536], P(('group', 'tensor')), may hold values from -0.09375 to 0.09375
- w_down: bfloat16 [128, 768, 4096], P(('group', 'tensor')), may hold values from -0.21875 to 0.21875
Outputs:
- layer_out: bfloat16 [4096, 4096], P(('group', 'tensor'))
Inputs may be any that keep to these rules, and one draw needn't show every extreme that they name: `document_index`: ids never fall along a group's tokens; equal ids mark one document. `expert_ids`: a token names 8 different experts; among the 32 tokens of one device (aligned blocks of rows) no expert is named more than 4 times, a bound that some block reaches.
All inputs are finite; a program needn't handle non-finite values.
Results may differ from a plain program's by a relative error of at most 0.0045.
Values may be sent and summed in bfloat16 or wider, within the bound.
No kernel may reach another device: no remote copies, remote signals or barrier semaphores. Data moves between devices by JAX's collectives and lax.ppermute only.
A program may use at most 128 MiB of HBM per device.

v0:
```python
import jax
import jax.numpy as jnp
from jax import lax
from jax.experimental import pallas as pl
from jax.experimental.pallas import tpu as pltpu
from jax.sharding import Mesh, PartitionSpec as P

HEAD_SIZE = 128
SLOTS = 4
VMEM = pltpu.VMEM
SMEM = pltpu.SMEM
F32 = jnp.float32
BF16 = jnp.bfloat16


def dot(a, b, dims=((1,), (0,))):
    return lax.dot_general(a, b, (dims, ((), ())), preferred_element_type=F32)


def vspec():
    return pl.BlockSpec(memory_space=VMEM)


def sspec():
    return pl.BlockSpec(memory_space=SMEM)


def call(body, outs, *args, flops=0, limit=8, out=True, hbm=(), scratch=()):
    specs, placed = [], []
    for a in args:
        if a.dtype == jnp.int32 and a.ndim == 1:
            specs.append(sspec())
            placed.append(a)
        elif any(a is h for h in hbm):
            specs.append(pl.BlockSpec(memory_space=pl.ANY))
            placed.append(pltpu.with_memory_space_constraint(a, pltpu.HBM))
        else:
            specs.append(vspec())
            placed.append(pltpu.with_memory_space_constraint(a, VMEM))
    single = not isinstance(outs, list)
    shapes = [outs] if single else outs
    out_shape = [VMEM(o.shape, o.dtype) for o in shapes] if out else shapes
    result = pl.pallas_call(
        body,
        out_shape=out_shape,
        in_specs=specs,
        out_specs=[vspec()] * len(shapes),
        scratch_shapes=list(scratch),
        compiler_params=pltpu.CompilerParams(vmem_limit_bytes=limit * 2**20),
        cost_estimate=pl.CostEstimate(flops=flops, bytes_accessed=0, transcendentals=0),
    )(*placed)
    return result[0] if single else result


def shape(dims, dtype):
    return jax.ShapeDtypeStruct(dims, dtype)


def ring(value, axis, shift, length):
    return lax.ppermute(value, axis, [(i, (i - shift) % length) for i in range(length)])


CHUNKS = 4


def attention_body(
    q_hbm, k_hbm, v_hbm, doc_hbm, up_hbm, out_ref, up_ref, q_ref, k_ref, v_ref, doc_ref, sems, load
):
    pairs = ((doc_hbm, doc_ref), (k_hbm, k_ref), (v_hbm, v_ref), (q_hbm, q_ref))
    copies = [pltpu.make_async_copy(h, v, sems.at[i]) for i, (h, v) in enumerate(pairs)]
    for copy in copies:
        copy.start()
    rows = up_ref.shape[0]
    wide = pltpu.make_async_copy(up_hbm.at[0, pl.ds(0, rows), :], up_ref, load)
    wide.start()
    for copy in copies:
        copy.wait()
    tokens = q_ref.shape[0]
    doc = jnp.broadcast_to(doc_ref[...].astype(F32), (tokens, tokens))
    row = lax.broadcasted_iota(jnp.int32, (tokens, tokens), 0)
    col = lax.broadcasted_iota(jnp.int32, (tokens, tokens), 1)
    visible = (row >= col) & (doc == doc.T)
    key = k_ref[...]
    value = v_ref[...]
    for h in range(q_ref.shape[1] // HEAD_SIZE):
        cols = slice(h * HEAD_SIZE, (h + 1) * HEAD_SIZE)
        scores = dot(q_ref[:, cols], key, ((1,), (1,))) * (1.0 / HEAD_SIZE**0.5)
        scores = jnp.where(visible, scores, -jnp.inf)
        top = jnp.max(scores, axis=-1, keepdims=True)
        exponent = jnp.where(visible, jnp.exp(scores - top), 0.0)
        probs = (exponent / jnp.sum(exponent, axis=-1, keepdims=True)).astype(BF16)
        out_ref[:, cols] = dot(probs, value).astype(BF16)
    wide.wait()


def join_body(a, b, c, d, out_ref):
    for i, ref in enumerate((a, b, c, d)):
        out_ref[:, i * 128 : (i + 1) * 128] = ref[...]


def project_body(own_ref, other_ref, *refs):
    z, c, y = lax.axis_index("z"), lax.axis_index("c"), lax.axis_index("y")
    pieces, outs = refs[:-4], refs[-4:]
    tok = pieces[0].shape[0] // 4
    wide = own_ref.shape[1] // 4
    own, other = own_ref[...], other_ref[...]
    for s, out_ref in enumerate(outs):
        rows = pl.ds(pl.multiple_of(lax.rem(y + s, 4) * tok, tok), tok)
        heads = jnp.concatenate([piece[rows, :] for piece in pieces], axis=0)
        for weight, core in ((own, c), (other, 1 - c)):
            part = dot(heads, weight).astype(BF16)
            for t in range(4):
                at = pl.multiple_of((lax.rem(z + t, 4) * 2 + core) * wide, wide)
                out_ref[:, pl.ds(at, wide)] = part[:, t * wide : (t + 1) * wide]


def total_body(a, b, c, d, *outs):
    tok = outs[0].shape[0]
    for i, out_ref in enumerate(outs):
        rows = slice(i * tok, (i + 1) * tok)
        total = a[rows, :].astype(F32) + b[rows, :].astype(F32)
        total = total + c[rows, :].astype(F32) + d[rows, :].astype(F32)
        out_ref[...] = total.astype(out_ref.dtype)


def norm_body(p0, p1, p2, p3, residual_ref, gain_ref, hidden_ref, normed_ref):
    x = lax.axis_index("x")
    tok, model = residual_ref.shape
    width = model // 4
    square = jnp.zeros((tok, 1), F32)
    for s, piece in enumerate((p0, p1, p2, p3)):
        cols = pl.ds(pl.multiple_of(lax.rem(x + 4 - s, 4) * width, width), width)
        total = residual_ref[:, cols].astype(F32) + piece[...].astype(F32)
        hidden_ref[:, cols] = total
        square = square + jnp.sum(total * total, axis=-1, keepdims=True)
    scale = lax.rsqrt(square * (1.0 / model) + 1e-06)
    normed_ref[...] = (hidden_ref[...] * scale * gain_ref[...]).astype(BF16)


def routing(core, ids, slots):
    tokens = ids.shape[0]
    half = tokens // 2
    slot = lax.broadcasted_iota(jnp.int32, (tokens, slots), 1)
    token = lax.broadcasted_iota(jnp.int32, (tokens, slots), 0)
    chip = slot // (2 * SLOTS)
    expert = ((chip // 4) * 2 + core) * 4 + chip % 4
    named = [ids[:, j : j + 1] == expert for j in range(ids.shape[1])]
    match = named[0]
    for one in named[1:]:
        match = match | one
    r = lax.broadcasted_iota(jnp.int32, (tokens, tokens), 0)
    c = lax.broadcasted_iota(jnp.int32, (tokens, tokens), 1)
    ahead = (c < r) & ((c < half) == (r < half))
    rank = dot(ahead.astype(BF16), match.astype(BF16)).astype(jnp.int32)
    here = match & (rank == slot % SLOTS) & ((token < half) == (slot % (2 * SLOTS) < SLOTS))
    return here, named


def expert_body(
    rows_ref, first_ref, up_hbm, down_ref, out_ref, sum_ref, second_ref, act_ref, sems
):
    tile, ff = act_ref.shape
    half = first_ref.shape[0]
    rows = half // CHUNKS
    copies = [
        pltpu.make_async_copy(
            up_hbm.at[0, pl.ds(half + i * rows, rows), :],
            second_ref.at[pl.ds(i * rows, rows), :],
            sems.at[i],
        )
        for i in range(CHUNKS)
    ]
    for copy in copies:
        copy.start()
    steps = rows_ref.shape[0] // tile

    def begin(m, carry):
        at = pl.ds(pl.multiple_of(m * tile, tile), tile)
        sum_ref[at, :] = dot(rows_ref[at, :half], first_ref[...])
        return carry

    def step(m, carry):
        at = pl.ds(pl.multiple_of(m * tile, tile), tile)
        right = rows_ref[at, half:]
        gate = sum_ref[at, :ff] + dot(right, second_ref[:, :ff])
        up = sum_ref[at, ff:] + dot(right, second_ref[:, ff:])
        act_ref[...] = (gate / (1.0 + jnp.exp(-gate)) * up).astype(BF16)
        out_ref[at, :] = dot(act_ref[...], down_ref[...]).astype(BF16)
        return carry

    lax.fori_loop(0, steps, begin, 0)
    for copy in copies:
        copy.wait()
    lax.fori_loop(0, steps, step, 0)


def pack_body(ids_ref, gates_ref, out_ref):
    top = ids_ref.shape[0]
    out_ref[:top] = ids_ref[...].astype(F32)
    out_ref[top:] = gates_ref[...]


def tables_body(own_ref, sibling_ref, table_ref, weights_ref):
    tokens, slots = table_ref.shape
    top = own_ref.shape[0] // 2
    route = jnp.concatenate([own_ref[...].T, sibling_ref[...].T], axis=0)
    ids = route[:, :top].astype(jnp.int32)
    gates = route[:, top:]
    here, named = routing(lax.axis_index("c"), ids, slots)
    weight = jnp.zeros(here.shape, F32)
    for j, one in enumerate(named):
        weight = weight + jnp.where(one, gates[:, j : j + 1], 0.0)
    weight = jnp.where(here, weight, 0.0)
    high = weight.astype(BF16)
    table_ref[...] = here.astype(BF16)
    weights_ref[:tokens] = high
    weights_ref[tokens:] = (weight - high.astype(F32)).astype(BF16)


def dispatch_body(table_ref, own_ref, other_ref, out_ref):
    tokens = jnp.concatenate([own_ref[...], other_ref[...]], axis=0)
    out_ref[...] = dot(table_ref[...], tokens, ((0,), (0,))).astype(BF16)


def combine_body(results_ref, weights_ref, hidden_ref, own_ref, other_ref):
    total = dot(weights_ref[...], results_ref[...])
    tok = hidden_ref.shape[0]
    other_ref[...] = total[tok : 2 * tok] + total[3 * tok :]
    own_ref[...] = hidden_ref[...] + (total[:tok] + total[2 * tok : 3 * tok])


def finish_body(own_ref, other_ref, out_ref):
    out_ref[...] = (own_ref[...] + other_ref[...]).astype(BF16)


def layer(
    queries,
    keys,
    values,
    document_index,
    out_proj,
    residual_in,
    norm_gain,
    expert_ids,
    gate_weights,
    w_gate_up,
    w_down,
):
    tok, model = residual_in.shape
    tokens, head_cols = queries.shape
    ff = w_down.shape[1]
    slots = 64 * 2 * SLOTS
    width = model // 4

    columns = [ring(out_proj, "z", s, 4) for s in (1, 2, 3)]
    inputs = (queries, keys, values, document_index)
    half_rows = shape((model // 2, 2 * ff), BF16)
    heads, first = call(
        attention_body, [shape((tokens, head_cols), BF16), half_rows],
        *inputs, w_gate_up, flops=10**10, hbm=(*inputs, w_gate_up),
        scratch=[VMEM(a.shape, a.dtype) for a in inputs]
        + [pltpu.SemaphoreType.DMA((4,)), pltpu.SemaphoreType.DMA(())],
    )
    near = [heads] + [ring(heads, "x", s, 4) for s in (1, 3)]
    far = [ring(heads, "x", 2, 4)]
    own_cols = call(
        join_body, shape((head_cols, model // 8), BF16),
        out_proj, *columns,
    )
    other_cols = ring(own_cols, "c", 1, 2)

    route = call(
        pack_body, shape((2 * expert_ids.shape[1], tok), F32),
        expert_ids.T, gate_weights.T,
    )
    sibling = ring(route, "c", 1, 2)
    table, weights = call(
        tables_body, [shape((2 * tok, slots), BF16), shape((4 * tok, slots), BF16)],
        route, sibling,
    )

    parts = {}
    for name, pieces in (("near", near), ("far", far)):
        outs = [shape((len(pieces) * tok, width), BF16)] * 4
        operands = (own_cols, other_cols, *pieces)
        mine, *sent = call(project_body, outs, *operands, flops=10**9)
        got = [ring(v, "y", -s, 4) for s, v in zip((1, 2, 3), sent)]
        kinds = [F32, BF16, BF16] if name == "near" else [BF16]
        sums = call(total_body, [shape((tok, width), k) for k in kinds], mine, *got)
        for s, v in zip((0, 1, 3) if name == "near" else (2,), sums):
            parts[s] = ring(v, "x", -s, 4) if s else v

    hidden, normed = call(
        norm_body, [shape((tok, model), F32), shape((tok, model), BF16)],
        *[parts[s] for s in range(4)], residual_in, norm_gain.reshape(1, model),
    )

    outgoing = call(
        dispatch_body, shape((slots, model), BF16),
        table, normed, ring(normed, "c", 1, 2),
    )
    rows = lax.all_to_all(
        outgoing.reshape(64, 2 * SLOTS, model), ("x", "z", "y"), 0, 0, tiled=True
    ).reshape(slots, model)

    expert_out = call(
        expert_body, shape((slots, model), BF16), rows, first, w_gate_up, w_down[0],
        flops=10**10, hbm=(w_gate_up,), limit=16,
        scratch=[
            VMEM((slots, 2 * ff), F32),
            VMEM(half_rows.shape, BF16),
            VMEM((256, ff), BF16),
            pltpu.SemaphoreType.DMA((CHUNKS,)),
        ],
    )
    results = lax.all_to_all(
        expert_out.reshape(64, 2 * SLOTS, model), ("x", "z", "y"), 0, 0, tiled=True
    ).reshape(slots, model)
    own, other = call(combine_body, [shape((tok, model), F32)] * 2, results, weights, hidden)
    return call(finish_body, shape((tok, model), BF16), own, ring(other, "c", 1, 2), out=False)


def solution(mesh):
    fine = Mesh(mesh.devices.reshape(4, 4, 2, 4), ("x", "z", "c", "y"))
    group = ("x", "z", "c")
    every = group + ("y",)
    in_specs = (
        P(group, "y"),
        P(group, "y"),
        P(group, "y"),
        P(group, None),
        P("y", group),
        P(every, None),
        P(),
        P(every, None),
        P(every, None),
        P(every, None, None),
        P(every, None, None),
    )
    return jax.shard_map(
        layer, mesh=fine, in_specs=in_specs, out_specs=P(every, None), check_vma=False
    )
```

profile of v0, /device:TPU:1, one launch (start us, length us, event | category | flops | bytes accessed | tf_op | source)
XLA Modules:
  0.0 202.3 jit_solution(10057826262017301621)
XLA Ops:
  0.0 4.4 %collective-permute-start.2 = (bf16[1024,128]{1,0:T(8,128)(2,1)}, bf16[1024,128]{1,0:T(8,128)(2,1)S(1)}, u32[]{:S(2)}, u32[]{:S(2)}) collective-permute-start(bf16[1024,128]{1,0:T(8,128)(2,1)} %a.1), channel_id=1, source_target_pairs={{0,16},{8,24},{16,0},{24,8},{1,17},{9,25},{17,1},{25,9},{2,18},{10... | collective-permute-start | bytes 786440 | tf_op jit(solution)/shard_map/ppermute | solution.py:60
  4.4 0.4 collective-permute-start.1
  4.8 1.0 collective-permute-start.3
  5.9 4.8 %collective-permute-done.2.c = bf16[1024,128]{1,0:T(8,128)(2,1)S(1)} collective-permute-done((bf16[1024,128]{1,0:T(8,128)(2,1)}, bf16[1024,128]{1,0:T(8,128)(2,1)S(1)}, u32[]{:S(2)}, u32[]{:S(2)}) %collective-permute-start.2) | collective-permute-done | bytes 262176 | tf_op jit(solution)/shard_map/ppermute | solution.py:60
  10.6 6.1 %collective-permute-done.1.b = bf16[1024,128]{1,0:T(8,128)(2,1)S(1)} collective-permute-done((bf16[1024,128]{1,0:T(8,128)(2,1)}, bf16[1024,128]{1,0:T(8,128)(2,1)S(1)}, u32[]{:S(2)}, u32[]{:S(2)}) %collective-permute-start.1) | collective-permute-done | bytes 262176 | tf_op jit(solution)/shard_map/ppermute | solution.py:60
  16.8 0.2 collective-permute-done.3.d
  17.0 0.9 copy-done.1
  18.0 0.2 shard_map.111.own_ref
  18.1 1.4 collective-permute-start.4
  19.5 3.7 %shard_map.112 = (bf16[128,1024]{1,0:T(8,128)(2,1)S(1)}, bf16[2048,1536]{1,0:T(8,128)(2,1)S(1)}) custom-call(bf16[128,1024]{1,0:T(8,128)(2,1)} %q_hbm.1, bf16[128,128]{1,0:T(8,128)(2,1)} %k_hbm.1, bf16[128,128]{1,0:T(8,128)(2,1)} %v_hbm.1, s32[1,128]{1,0:T(1,128)} %doc_hbm.1, bf16[1,4096,1536]{2,1,0:T(8,128)(2,1)} %up_hbm.3), custom_call_target="tpu_custom_call" | custom-call | flops 10000000000 | tf_op jit(solution)/shard_map/pallas_call | solution.py:43
  23.2 0.0 copy-start
  23.3 0.0 copy-start.2
  23.3 0.0 copy-start.3
  23.3 0.0 copy-start.4
  23.3 1.3 collective-permute-start.6
  24.6 1.5 collective-permute-start.5
  26.0 1.5 collective-permute-start.11
  27.6 4.8 %collective-permute-done.6.refs_2_ = bf16[128,1024]{1,0:T(8,128)(2,1)S(1)} collective-permute-done((bf16[128,1024]{1,0:T(8,128)(2,1)S(1)}, bf16[128,1024]{1,0:T(8,128)(2,1)S(1)}, u32[]{:S(2)}, u32[]{:S(2)}) %collective-permute-start.6) | collective-permute-done | bytes 262176 | tf_op jit(solution)/shard_map/ppermute | solution.py:60
  32.4 0.0 collective-permute-done.5.refs_1_
  32.4 0.0 collective-permute-done.4.other_ref
  32.4 1.5 shard_map.113
  33.9 1.4 collective-permute-start.7
  35.3 2.6 %collective-permute-start.8 = (bf16[96,1024]{1,0:T(8,128)(2,1)S(1)}, bf16[96,1024]{1,0:T(8,128)(2,1)S(1)}, u32[]{:S(2)}, u32[]{:S(2)}) collective-permute-start(bf16[96,1024]{1,0:T(8,128)(2,1)S(1)} %get-tuple-element.28), channel_id=1, source_target_pairs={{0,2},{1,3},{2,0},{3,1},{4,6},{5,7},{6,4},{7,5},{8,10},{9,11},{10,... | collective-permute-start | bytes 589832 | tf_op jit(solution)/shard_map/ppermute | solution.py:60
  37.9 1.1 collective-permute-start.9
  39.0 0.1 collective-permute-done.11.refs_0_
  39.0 1.5 shard_map.115
  40.6 1.4 collective-permute-start.12
  41.9 2.6 %collective-permute-start.13 = (bf16[32,1024]{1,0:T(8,128)(2,1)S(1)}, bf16[32,1024]{1,0:T(8,128)(2,1)S(1)}, u32[]{:S(2)}, u32[]{:S(2)}) collective-permute-start(bf16[32,1024]{1,0:T(8,128)(2,1)S(1)} %get-tuple-element.34), channel_id=1, source_target_pairs={{0,2},{1,3},{2,0},{3,1},{4,6},{5,7},{6,4},{7,5},{8,10},{9,11},{10,... | collective-permute-start | bytes 196616 | tf_op jit(solution)/shard_map/ppermute | solution.py:60
  44.5 1.5 collective-permute-done.12.b
  46.0 1.5 collective-permute-start.14
  47.5 0.8 collective-permute-done.13.c
  48.3 1.8 collective-permute-done.14.d
  50.2 0.9 collective-permute-start.15
  51.1 0.0 collective-permute-done.7.b
  51.1 0.0 collective-permute-done.8.c
  51.1 0.0 collective-permute-done.9.d
  51.1 0.1 shard_map.114
  51.2 2.7 %collective-permute-start.10 = (bf16[32,1024]{1,0:T(8,128)(2,1)S(1)}, bf16[32,1024]{1,0:T(8,128)(2,1)S(1)}, u32[]{:S(2)}, u32[]{:S(2)}) collective-permute-start(bf16[32,1024]{1,0:T(8,128)(2,1)S(1)} %get-tuple-element.31), channel_id=1, source_target_pairs={{0,32},{32,64},{64,96},{96,0},{1,33},{33,65},{65,97},{97,1},{2,34}... | collective-permute-start | bytes 196616 | tf_op jit(solution)/shard_map/ppermute | solution.py:60
  53.9 0.1 collective-permute-start.16
  54.0 0.9 collective-permute-done.15.p2
  54.9 0.8 collective-permute-done.10.p1
  55.6 1.4 collective-permute-done.16.p3
  57.0 0.0 copy-done
  57.0 0.0 copy-done.2
  57.0 0.2 shard_map.117
  57.2 9.1 %collective-permute-start.17 = (bf16[32,4096]{1,0:T(8,128)(2,1)S(1)}, bf16[32,4096]{1,0:T(8,128)(2,1)S(1)}, u32[]{:S(2)}, u32[]{:S(2)}) collective-permute-start(bf16[32,4096]{1,0:T(8,128)(2,1)S(1)} %get-tuple-element.37.own_ref), channel_id=1, source_target_pairs={{0,4},{4,0},{1,5},{5,1},{2,6},{6,2},{3,7},{7,3},{8,12},{12,8},{9,1... | collective-permute-start | bytes 786440 | tf_op jit(solution)/shard_map/ppermute | solution.py:60
  66.4 0.0 copy-done.3
  66.4 0.0 copy-done.4
  66.4 0.1 collective-permute-start
  66.5 1.1 collective-permute-done.sibling_ref
  67.6 0.5 shard_map.110
  68.1 0.0 collective-permute-done.17.other_ref
  68.1 0.0 slice-start
  68.2 1.3 shard_map.118
  69.4 0.0 slice-start.1
  69.5 55.9 %all_to_all.10 = bf16[64,8,4096]{2,1,0:T(8,128)(2,1)S(1)} all-to-all(bf16[64,8,4096]{2,1,0:T(8,128)(2,1)S(1)} %bitcast.9), channel_id=1, replica_groups=mesh['x'=4,'z'=4,'c'=2,'y'=4] {'x','z','y'}, dimensions={0} | all-to-all | bytes 8388608 | tf_op jit(solution)/shard_map/all_to_all | solution.py:302
  125.4 0.0 slice-done
  125.4 0.0 slice-done.1
  125.4 10.5 %shard_map.119 = bf16[512,4096]{1,0:T(8,128)(2,1)S(1)} custom-call(bf16[512,4096]{1,0:T(8,128)(2,1)S(1)} %bitcast.10, bf16[2048,1536]{1,0:T(8,128)(2,1)S(1)} %get-tuple-element.38.first_ref, bf16[1,4096,1536]{2,1,0:T(8,128)(2,1)} %up_hbm.3, bf16[768,4096]{1,0:T(8,128)(2,1)S(1)} %bitcast.17), custom_call_target="tpu_custom_call" | custom-call | flops 10000000000 | tf_op jit(solution)/shard_map/pallas_call | solution.py:43
  135.9 59.6 %all_to_all.11 = bf16[64,8,4096]{2,1,0:T(8,128)(2,1)S(1)} all-to-all(bf16[64,8,4096]{2,1,0:T(8,128)(2,1)S(1)} %bitcast.11), channel_id=1, replica_groups=mesh['x'=4,'z'=4,'c'=2,'y'=4] {'x','z','y'}, dimensions={0} | all-to-all | bytes 8388608 | tf_op jit(solution)/shard_map/all_to_all | solution.py:316
  195.5 0.7 shard_map.120
  196.2 3.8 %collective-permute-start.18 = (f32[32,4096]{1,0:T(8,128)S(1)}, f32[32,4096]{1,0:T(8,128)S(1)}, u32[]{:S(2)}, u32[]{:S(2)}) collective-permute-start(f32[32,4096]{1,0:T(8,128)S(1)} %get-tuple-element.42), channel_id=1, source_target_pairs={{0,4},{4,0},{1,5},{5,1},{2,6},{6,2},{3,7},{7,3},{8,12},{12,8},{9,1... | collective-permute-start | bytes 1572872 | tf_op jit(solution)/shard_map/ppermute | solution.py:60
  200.0 1.5 collective-permute-done.18.other_ref
  201.5 0.7 shard_map.121
  (4 shorter events, 0.0 us)
Async XLA Ops:
  0.0 10.6 %collective-permute-start.2 = (bf16[1024,128]{1,0:T(8,128)(2,1)}, bf16[1024,128]{1,0:T(8,128)(2,1)S(1)}, u32[]{:S(2)}, u32[]{:S(2)}) collective-permute-start(bf16[1024,128]{1,0:T(8,128)(2,1)} %a.1), channel_id=1, source_target_pairs={{0,16},{8,24},{16,0},{24,8},{1,17},{9,25},{17,1},{25,9},{2,18},{10... | collective-permute-start | bytes 786440 | tf_op jit(solution)/shard_map/ppermute | solution.py:60
  4.4 12.4 %collective-permute-start.1 = (bf16[1024,128]{1,0:T(8,128)(2,1)}, bf16[1024,128]{1,0:T(8,128)(2,1)S(1)}, u32[]{:S(2)}, u32[]{:S(2)}) collective-permute-start(bf16[1024,128]{1,0:T(8,128)(2,1)} %a.1), channel_id=1, source_target_pairs={{0,24},{8,0},{16,8},{24,16},{1,25},{9,1},{17,9},{25,17},{2,26},{10... | collective-permute-start | bytes 786440 | tf_op jit(solution)/shard_map/ppermute | solution.py:60
  4.8 12.2 %collective-permute-start.3 = (bf16[1024,128]{1,0:T(8,128)(2,1)}, bf16[1024,128]{1,0:T(8,128)(2,1)S(1)}, u32[]{:S(2)}, u32[]{:S(2)}) collective-permute-start(bf16[1024,128]{1,0:T(8,128)(2,1)} %a.1), channel_id=1, source_target_pairs={{0,8},{8,16},{16,24},{24,0},{1,9},{9,17},{17,25},{25,1},{2,10},{10... | collective-permute-start | bytes 786440 | tf_op jit(solution)/shard_map/ppermute | solution.py:60
  17.0 1.0 copy-start.1
  18.1 14.3 %collective-permute-start.4 = (bf16[1024,512]{1,0:T(8,128)(2,1)S(1)}, bf16[1024,512]{1,0:T(8,128)(2,1)S(1)}, u32[]{:S(2)}, u32[]{:S(2)}) collective-permute-start(bf16[1024,512]{1,0:T(8,128)(2,1)S(1)} %shard_map.111.own_ref), channel_id=1, source_target_pairs={{0,4},{4,0},{1,5},{5,1},{2,6},{6,2},{3,7},{7,3},{8,12},{12,8},{9,1... | collective-permute-start | bytes 3145736 | tf_op jit(solution)/shard_map/ppermute | solution.py:60
  23.2 33.8 %copy-start = (bf16[32,4096]{1,0:T(8,128)(2,1)S(1)}, bf16[32,4096]{1,0:T(8,128)(2,1)}, u32[]{:S(2)}) copy-start(bf16[32,4096]{1,0:T(8,128)(2,1)} %residual_ref.1) | copy-start | bytes 786436
  23.3 33.8 %copy-start.2 = (f32[4096]{0:T(1024)S(1)}, f32[4096]{0:T(1024)}, u32[]{:S(2)}) copy-start(f32[4096]{0:T(1024)} %param.17) | copy-start | bytes 49156
  23.3 43.1 %copy-start.3 = (s32[32,8]{0,1:T(8,128)S(1)}, s32[32,8]{0,1:T(8,128)}, u32[]{:S(2)}) copy-start(s32[32,8]{0,1:T(8,128)} %param.18) | copy-start | bytes 3076
  23.3 43.1 %copy-start.4 = (f32[32,8]{0,1:T(8,128)S(1)}, f32[32,8]{0,1:T(8,128)}, u32[]{:S(2)}) copy-start(f32[32,8]{0,1:T(8,128)} %param.19) | copy-start | bytes 3076
  23.3 9.1 %collective-permute-start.6 = (bf16[128,1024]{1,0:T(8,128)(2,1)S(1)}, bf16[128,1024]{1,0:T(8,128)(2,1)S(1)}, u32[]{:S(2)}, u32[]{:S(2)}) collective-permute-start(bf16[128,1024]{1,0:T(8,128)(2,1)S(1)} %get-tuple-element.25.refs_0_), channel_id=1, source_target_pairs={{0,32},{32,64},{64,96},{96,0},{1,33},{33,65},{65,97},{97,1},{2,34}... | collective-permute-start | bytes 786440 | tf_op jit(solution)/shard_map/ppermute | solution.py:60
  24.6 7.8 %collective-permute-start.5 = (bf16[128,1024]{1,0:T(8,128)(2,1)S(1)}, bf16[128,1024]{1,0:T(8,128)(2,1)S(1)}, u32[]{:S(2)}, u32[]{:S(2)}) collective-permute-start(bf16[128,1024]{1,0:T(8,128)(2,1)S(1)} %get-tuple-element.25.refs_0_), channel_id=1, source_target_pairs={{0,96},{32,0},{64,32},{96,64},{1,97},{33,1},{65,33},{97,65},{2,98}... | collective-permute-start | bytes 786440 | tf_op jit(solution)/shard_map/ppermute | solution.py:60
  26.0 13.0 %collective-permute-start.11 = (bf16[128,1024]{1,0:T(8,128)(2,1)S(1)}, bf16[128,1024]{1,0:T(8,128)(2,1)S(1)}, u32[]{:S(2)}, u32[]{:S(2)}) collective-permute-start(bf16[128,1024]{1,0:T(8,128)(2,1)S(1)} %get-tuple-element.25.refs_0_), channel_id=1, source_target_pairs={{0,64},{32,96},{64,0},{96,32},{1,65},{33,97},{65,1},{97,33},{2,66}... | collective-permute-start | bytes 786440 | tf_op jit(solution)/shard_map/ppermute | solution.py:60
  33.9 17.2 %collective-permute-start.7 = (bf16[96,1024]{1,0:T(8,128)(2,1)S(1)}, bf16[96,1024]{1,0:T(8,128)(2,1)S(1)}, u32[]{:S(2)}, u32[]{:S(2)}) collective-permute-start(bf16[96,1024]{1,0:T(8,128)(2,1)S(1)} %get-tuple-element.27), channel_id=1, source_target_pairs={{0,1},{1,2},{2,3},{3,0},{4,5},{5,6},{6,7},{7,4},{8,9},{9,10},{10,1... | collective-permute-start | bytes 589832 | tf_op jit(solution)/shard_map/ppermute | solution.py:60
  35.3 15.8 %collective-permute-start.8 = (bf16[96,1024]{1,0:T(8,128)(2,1)S(1)}, bf16[96,1024]{1,0:T(8,128)(2,1)S(1)}, u32[]{:S(2)}, u32[]{:S(2)}) collective-permute-start(bf16[96,1024]{1,0:T(8,128)(2,1)S(1)} %get-tuple-element.28), channel_id=1, source_target_pairs={{0,2},{1,3},{2,0},{3,1},{4,6},{5,7},{6,4},{7,5},{8,10},{9,11},{10,... | collective-permute-start | bytes 589832 | tf_op jit(solution)/shard_map/ppermute | solution.py:60
  37.9 13.2 %collective-permute-start.9 = (bf16[96,1024]{1,0:T(8,128)(2,1)S(1)}, bf16[96,1024]{1,0:T(8,128)(2,1)S(1)}, u32[]{:S(2)}, u32[]{:S(2)}) collective-permute-start(bf16[96,1024]{1,0:T(8,128)(2,1)S(1)} %get-tuple-element.29), channel_id=1, source_target_pairs={{0,3},{1,0},{2,1},{3,2},{4,7},{5,4},{6,5},{7,6},{8,11},{9,8},{10,9... | collective-permute-start | bytes 589832 | tf_op jit(solution)/shard_map/ppermute | solution.py:60
  40.6 5.4 %collective-permute-start.12 = (bf16[32,1024]{1,0:T(8,128)(2,1)S(1)}, bf16[32,1024]{1,0:T(8,128)(2,1)S(1)}, u32[]{:S(2)}, u32[]{:S(2)}) collective-permute-start(bf16[32,1024]{1,0:T(8,128)(2,1)S(1)} %get-tuple-element.33), channel_id=1, source_target_pairs={{0,1},{1,2},{2,3},{3,0},{4,5},{5,6},{6,7},{7,4},{8,9},{9,10},{10,1... | collective-permute-start | bytes 196616 | tf_op jit(solution)/shard_map/ppermute | solution.py:60
  41.9 6.4 %collective-permute-start.13 = (bf16[32,1024]{1,0:T(8,128)(2,1)S(1)}, bf16[32,1024]{1,0:T(8,128)(2,1)S(1)}, u32[]{:S(2)}, u32[]{:S(2)}) collective-permute-start(bf16[32,1024]{1,0:T(8,128)(2,1)S(1)} %get-tuple-element.34), channel_id=1, source_target_pairs={{0,2},{1,3},{2,0},{3,1},{4,6},{5,7},{6,4},{7,5},{8,10},{9,11},{10,... | collective-permute-start | bytes 196616 | tf_op jit(solution)/shard_map/ppermute | solution.py:60
  46.0 4.1 %collective-permute-start.14 = (bf16[32,1024]{1,0:T(8,128)(2,1)S(1)}, bf16[32,1024]{1,0:T(8,128)(2,1)S(1)}, u32[]{:S(2)}, u32[]{:S(2)}) collective-permute-start(bf16[32,1024]{1,0:T(8,128)(2,1)S(1)} %get-tuple-element.35), channel_id=1, source_target_pairs={{0,3},{1,0},{2,1},{3,2},{4,7},{5,4},{6,5},{7,6},{8,11},{9,8},{10,9... | collective-permute-start | bytes 196616 | tf_op jit(solution)/shard_map/ppermute | solution.py:60
  50.2 4.7 %collective-permute-start.15 = (bf16[32,1024]{1,0:T(8,128)(2,1)S(1)}, bf16[32,1024]{1,0:T(8,128)(2,1)S(1)}, u32[]{:S(2)}, u32[]{:S(2)}) collective-permute-start(bf16[32,1024]{1,0:T(8,128)(2,1)S(1)} %shard_map.116), channel_id=1, source_target_pairs={{0,64},{32,96},{64,0},{96,32},{1,65},{33,97},{65,1},{97,33},{2,66}... | collective-permute-start | bytes 196616 | tf_op jit(solution)/shard_map/ppermute | solution.py:60
  51.2 4.4 %collective-permute-start.10 = (bf16[32,1024]{1,0:T(8,128)(2,1)S(1)}, bf16[32,1024]{1,0:T(8,128)(2,1)S(1)}, u32[]{:S(2)}, u32[]{:S(2)}) collective-permute-start(bf16[32,1024]{1,0:T(8,128)(2,1)S(1)} %get-tuple-element.31), channel_id=1, source_target_pairs={{0,32},{32,64},{64,96},{96,0},{1,33},{33,65},{65,97},{97,1},{2,34}... | collective-permute-start | bytes 196616 | tf_op jit(solution)/shard_map/ppermute | solution.py:60
  53.9 3.1 %collective-permute-start.16 = (bf16[32,1024]{1,0:T(8,128)(2,1)S(1)}, bf16[32,1024]{1,0:T(8,128)(2,1)S(1)}, u32[]{:S(2)}, u32[]{:S(2)}) collective-permute-start(bf16[32,1024]{1,0:T(8,128)(2,1)S(1)} %get-tuple-element.36), channel_id=1, source_target_pairs={{0,96},{32,0},{64,32},{96,64},{1,97},{33,1},{65,33},{97,65},{2,98}... | collective-permute-start | bytes 196616 | tf_op jit(solution)/shard_map/ppermute | solution.py:60
  57.2 10.9 %collective-permute-start.17 = (bf16[32,4096]{1,0:T(8,128)(2,1)S(1)}, bf16[32,4096]{1,0:T(8,128)(2,1)S(1)}, u32[]{:S(2)}, u32[]{:S(2)}) collective-permute-start(bf16[32,4096]{1,0:T(8,128)(2,1)S(1)} %get-tuple-element.37.own_ref), channel_id=1, source_target_pairs={{0,4},{4,0},{1,5},{5,1},{2,6},{6,2},{3,7},{7,3},{8,12},{12,8},{9,1... | collective-permute-start | bytes 786440 | tf_op jit(solution)/shard_map/ppermute | solution.py:60
  66.4 1.3 collective-permute-start
  68.1 57.2 %slice-start = ((s8[6291456]{0:T(1024)(128)(4,1)}), s8[4194304]{0:T(1024)(128)(4,1)S(1)}, s32[]{:S(2)}) async-start(s8[6291456]{0:T(1024)(128)(4,1)} %bitcast.15), calls=%async_computation.2 | async-start | bytes 8388608
  69.4 55.9 %slice-start.1 = ((s8[6291456]{0:T(1024)(128)(4,1)}), s8[2097152]{0:T(1024)(128)(4,1)S(1)}, s32[]{:S(2)}) async-start(s8[6291456]{0:T(1024)(128)(4,1)} %bitcast.15), calls=%async_computation.3 | async-start | bytes 4194304
  196.2 5.3 %collective-permute-start.18 = (f32[32,4096]{1,0:T(8,128)S(1)}, f32[32,4096]{1,0:T(8,128)S(1)}, u32[]{:S(2)}, u32[]{:S(2)}) collective-permute-start(f32[32,4096]{1,0:T(8,128)S(1)} %get-tuple-element.42), channel_id=1, source_target_pairs={{0,4},{4,0},{1,5},{5,1},{2,6},{6,2},{3,7},{7,3},{8,12},{12,8},{9,1... | collective-permute-start | bytes 1572872 | tf_op jit(solution)/shard_map/ppermute | solution.py:60
where the time goes:
time: 202 us
  blocking collectives  116 us (57%)
  starting transfers between devices  38.7 us (19%)
  waiting for transfers between devices  25.9 us (13%)
  Pallas kernels  21 us (10%)
    all_to_all x1, blocking collectives, layer(): lax.all_to_all(expert_out.reshape(64, 2 * SLOTS, model), ('x', 'z', 'y'),...  59.6 us
    all_to_all x1, blocking collectives, layer(): lax.all_to_all(outgoing.reshape(64, 2 * SLOTS, model), ('x', 'z', 'y'), 0...  55.9 us
    ppermute x19, starting transfers between devices, ring(): lax.ppermute(value, axis, [(i, (i - shift) % length) for i in range(lengt...  38.7 us
    ppermute x19, waiting for transfers between devices, ring(): lax.ppermute(value, axis, [(i, (i - shift) % length) for i in range(lengt...  25.9 us
    pallas_call x13, Pallas kernels, call(): pl.pallas_call(body, out_shape=out_shape, in_specs=specs, out_specs=[vspe...  21 us
  transfers between devices with their start and end apart: 19, of which 13 were waited for; matrix products, arithmetic and copies ran while one was open for 0% of the time, Pallas kernels for 4%

commit v1 on v0

--- a/solution.py
+++ b/solution.py
@@ -58,9 +58,6 @@
 
 def ring(value, axis, shift, length):
     return lax.ppermute(value, axis, [(i, (i - shift) % length) for i in range(length)])
-
-
-CHUNKS = 4
 
 
 def attention_body(
@@ -156,42 +153,27 @@
     return here, named
 
 
-def expert_body(
-    rows_ref, first_ref, up_hbm, down_ref, out_ref, sum_ref, second_ref, act_ref, sems
-):
+def load_body(source, out_ref, sem):
+    rows = out_ref.shape[0]
+    copy = pltpu.make_async_copy(source.at[0, pl.ds(rows, rows), :], out_ref, sem)
+    copy.start()
+    copy.wait()
+
+
+def expert_body(rows_ref, first_ref, second_ref, down_ref, out_ref, act_ref):
     tile, ff = act_ref.shape
     half = first_ref.shape[0]
-    rows = half // CHUNKS
-    copies = [
-        pltpu.make_async_copy(
-            up_hbm.at[0, pl.ds(half + i * rows, rows), :],
-            second_ref.at[pl.ds(i * rows, rows), :],
-            sems.at[i],
-        )
-        for i in range(CHUNKS)
-    ]
-    for copy in copies:
-        copy.start()
-    steps = rows_ref.shape[0] // tile
-
-    def begin(m, carry):
-        at = pl.ds(pl.multiple_of(m * tile, tile), tile)
-        sum_ref[at, :] = dot(rows_ref[at, :half], first_ref[...])
-        return carry
 
     def step(m, carry):
         at = pl.ds(pl.multiple_of(m * tile, tile), tile)
-        right = rows_ref[at, half:]
-        gate = sum_ref[at, :ff] + dot(right, second_ref[:, :ff])
-        up = sum_ref[at, ff:] + dot(right, second_ref[:, ff:])
+        left, right = rows_ref[at, :half], rows_ref[at, half:]
+        gate = dot(left, first_ref[:, :ff]) + dot(right, second_ref[:, :ff])
+        up = dot(left, first_ref[:, ff:]) + dot(right, second_ref[:, ff:])
         act_ref[...] = (gate / (1.0 + jnp.exp(-gate)) * up).astype(BF16)
         out_ref[at, :] = dot(act_ref[...], down_ref[...]).astype(BF16)
         return carry
 
-    lax.fori_loop(0, steps, begin, 0)
-    for copy in copies:
-        copy.wait()
-    lax.fori_loop(0, steps, step, 0)
+    lax.fori_loop(0, rows_ref.shape[0] // tile, step, 0)
 
 
 def pack_body(ids_ref, gates_ref, out_ref):
@@ -263,6 +245,10 @@
     )
     near = [heads] + [ring(heads, "x", s, 4) for s in (1, 3)]
     far = [ring(heads, "x", 2, 4)]
+    second = call(
+        load_body, half_rows, w_gate_up, hbm=(w_gate_up,), flops=10**9,
+        scratch=[pltpu.SemaphoreType.DMA(())],
+    )
     own_cols = call(
         join_body, shape((head_cols, model // 8), BF16),
         out_proj, *columns,
@@ -284,7 +270,8 @@
         outs = [shape((len(pieces) * tok, width), BF16)] * 4
         operands = (own_cols, other_cols, *pieces)
         mine, *sent = call(project_body, outs, *operands, flops=10**9)
-        got = [ring(v, "y", -s, 4) for s, v in zip((1, 2, 3), sent)]
+        across = ring(sent[1], "y", -2, 4)
+        got = [across, ring(sent[0], "y", -1, 4), ring(sent[2], "y", -3, 4)]
         kinds = [F32, BF16, BF16] if name == "near" else [BF16]
         sums = call(total_body, [shape((tok, width), k) for k in kinds], mine, *got)
         for s, v in zip((0, 1, 3) if name == "near" else (2,), sums):
@@ -304,14 +291,8 @@
     ).reshape(slots, model)
 
     expert_out = call(
-        expert_body, shape((slots, model), BF16), rows, first, w_gate_up, w_down[0],
-        flops=10**10, hbm=(w_gate_up,), limit=16,
-        scratch=[
-            VMEM((slots, 2 * ff), F32),
-            VMEM(half_rows.shape, BF16),
-            VMEM((256, ff), BF16),
-            pltpu.SemaphoreType.DMA((CHUNKS,)),
-        ],
+        expert_body, shape((slots, model), BF16), rows, first, second, w_down[0],
+        flops=10**10, scratch=[VMEM((256, ff), BF16)],
     )
     results = lax.all_to_all(
         expert_out.reshape(64, 2 * SLOTS, model), ("x", "z", "y"), 0, 0, tiled=True

time: 202 us -> 229 us (1.13)
  waiting for transfers between devices: 25.9 us -> 86 us
  blocking collectives: 116 us -> 62.1 us
  local copies, waits for them, and re-layouts: 0.99 us -> 16.5 us
  Pallas kernels: 21 us -> 25.6 us
    all_to_all x1 -> x0, blocking collectives: 55.9 us -> none  [layer(): lax.all_to_all(outgoing.reshape(64, 2 * SLOTS, model), ('x', 'z', 'y'), 0...]
    all_to_all x0 -> x1, waiting for transfers between devices: none -> 47.9 us  [layer(): lax.all_to_all(outgoing.reshape(64, 2 * SLOTS, model), ('x', 'z', 'y'), 0...]
    unnamed x14 -> x22, local copies, waits for them, and re-layouts: 0.99 us -> 16.5 us
    ppermute x19, waiting for transfers between devices: 25.9 us -> 38.1 us  [ring(): lax.ppermute(value, axis, [(i, (i - shift) % length) for i in range(lengt...]
    ppermute x19, starting transfers between devices: 38.7 us -> 29.9 us  [ring(): lax.ppermute(value, axis, [(i, (i - shift) % length) for i in range(lengt...]
    all_to_all x0 -> x1, starting transfers between devices: none -> 8.17 us  [layer(): lax.all_to_all(outgoing.reshape(64, 2 * SLOTS, model), ('x', 'z', 'y'), 0...]
    pallas_call x13 -> x14, Pallas kernels: 21 us -> 25.6 us  [call(): pl.pallas_call(body, out_shape=out_shape, in_specs=specs, out_specs=[vspe...]
    all_to_all x1, blocking collectives: 59.6 us -> 62.1 us  [layer(): lax.all_to_all(expert_out.reshape(64, 2 * SLOTS, model), ('x', 'z', 'y'),...]
  transfers between devices with their start and end apart: 19 -> 20, of which waited for: 13 -> 11; matrix products, arithmetic and copies ran while one was open for 0% -> 0% of each run, Pallas kernels for 4% -> 4%
where the time goes in v1:
time: 229 us; the launch traced here: 228 us
  waiting for transfers between devices  86 us (38%)
  blocking collectives  62.1 us (27%)
  starting transfers between devices  38 us (17%)
  Pallas kernels  25.6 us (11%)
  local copies, waits for them, and re-layouts  16.5 us (7%)
    all_to_all x1, blocking collectives, layer(): lax.all_to_all(expert_out.reshape(64, 2 * SLOTS, model), ('x', 'z', 'y'),...  62.1 us
    all_to_all x1, waiting for transfers between devices, layer(): lax.all_to_all(outgoing.reshape(64, 2 * SLOTS, model), ('x', 'z', 'y'), 0...  47.9 us
    ppermute x19, waiting for transfers between devices, ring(): lax.ppermute(value, axis, [(i, (i - shift) % length) for i in range(lengt...  38.1 us
    ppermute x19, starting transfers between devices, ring(): lax.ppermute(value, axis, [(i, (i - shift) % length) for i in range(lengt...  29.9 us
    pallas_call x14, Pallas kernels, call(): pl.pallas_call(body, out_shape=out_shape, in_specs=specs, out_specs=[vspe...  25.6 us
    unnamed x22, local copies, waits for them, and re-layouts  16.5 us
    all_to_all x1, starting transfers between devices, layer(): lax.all_to_all(outgoing.reshape(64, 2 * SLOTS, model), ('x', 'z', 'y'), 0...  8.17 us
  transfers between devices with their start and end apart: 20, of which 11 were waited for; matrix products, arithmetic and copies ran while one was open for 0% of the time, Pallas kernels for 4%

profile of v1, /device:TPU:1, one launch (start us, length us, event | category | flops | bytes accessed | tf_op | source)
XLA Modules:
  0.0 228.5 jit_solution(2902703280425626706)
XLA Ops:
  0.0 4.6 %collective-permute-start.1 = (bf16[1024,128]{1,0:T(8,128)(2,1)}, bf16[1024,128]{1,0:T(8,128)(2,1)S(1)}, u32[]{:S(2)}, u32[]{:S(2)}) collective-permute-start(bf16[1024,128]{1,0:T(8,128)(2,1)} %a.1), channel_id=1, source_target_pairs={{0,24},{8,0},{16,8},{24,16},{1,25},{9,1},{17,9},{25,17},{2,26},{10... | collective-permute-start | bytes 786440 | tf_op jit(solution)/shard_map/ppermute | solution.py:60
  4.6 0.0 collective-permute-start.2
  4.6 0.7 collective-permute-start.3
  5.3 10.1 %collective-permute-done.1.b = bf16[1024,128]{1,0:T(8,128)(2,1)S(1)} collective-permute-done((bf16[1024,128]{1,0:T(8,128)(2,1)}, bf16[1024,128]{1,0:T(8,128)(2,1)S(1)}, u32[]{:S(2)}, u32[]{:S(2)}) %collective-permute-start.1) | collective-permute-done | bytes 262176 | tf_op jit(solution)/shard_map/ppermute | solution.py:60
  15.4 0.0 collective-permute-done.2.c
  15.4 4.2 %collective-permute-done.3.d = bf16[1024,128]{1,0:T(8,128)(2,1)S(1)} collective-permute-done((bf16[1024,128]{1,0:T(8,128)(2,1)}, bf16[1024,128]{1,0:T(8,128)(2,1)S(1)}, u32[]{:S(2)}, u32[]{:S(2)}) %collective-permute-start.3) | collective-permute-done | bytes 262176 | tf_op jit(solution)/shard_map/ppermute | solution.py:60
  19.6 0.9 copy-done.4
  20.5 0.2 shard_map.111.own_ref
  20.7 0.9 collective-permute-start.4
  21.6 3.7 %shard_map.112 = (bf16[128,1024]{1,0:T(8,128)(2,1)S(1)}, bf16[2048,1536]{1,0:T(8,128)(2,1)S(1)}) custom-call(bf16[128,1024]{1,0:T(8,128)(2,1)} %q_hbm.1, bf16[128,128]{1,0:T(8,128)(2,1)} %k_hbm.1, bf16[128,128]{1,0:T(8,128)(2,1)} %v_hbm.1, s32[1,128]{1,0:T(1,128)} %doc_hbm.1, bf16[1,4096,1536]{2,1,0:T(8,128)(2,1)} %source.1), custom_call_target="tpu_custom_call" | custom-call | flops 10000000000 | tf_op jit(solution)/shard_map/pallas_call | solution.py:43
  25.3 0.0 copy-start.9
  25.3 2.6 %copy-done.9 = bf16[2048,1536]{1,0:T(8,128)(2,1)} copy-done((bf16[2048,1536]{1,0:T(8,128)(2,1)}, bf16[2048,1536]{1,0:T(8,128)(2,1)S(1)}, u32[]{:S(2)}) %copy-start.9) | copy-done | bytes 6291480
  27.9 2.5 %collective-permute-start.5 = (bf16[128,1024]{1,0:T(8,128)(2,1)S(1)}, bf16[128,1024]{1,0:T(8,128)(2,1)S(1)}, u32[]{:S(2)}, u32[]{:S(2)}) collective-permute-start(bf16[128,1024]{1,0:T(8,128)(2,1)S(1)} %get-tuple-element.25.refs_0_), channel_id=1, source_target_pairs={{0,96},{32,0},{64,32},{96,64},{1,97},{33,1},{65,33},{97,65},{2,98}... | collective-permute-start | bytes 786440 | tf_op jit(solution)/shard_map/ppermute | solution.py:60
  30.5 0.0 collective-permute-start.6
  30.5 1.7 collective-permute-start.11
  32.2 9.4 %collective-permute-done.5.refs_1_ = bf16[128,1024]{1,0:T(8,128)(2,1)S(1)} collective-permute-done((bf16[128,1024]{1,0:T(8,128)(2,1)S(1)}, bf16[128,1024]{1,0:T(8,128)(2,1)S(1)}, u32[]{:S(2)}, u32[]{:S(2)}) %collective-permute-start.5) | collective-permute-done | bytes 262176 | tf_op jit(solution)/shard_map/ppermute | solution.py:60
  41.6 3.3 %collective-permute-done.6.refs_2_ = bf16[128,1024]{1,0:T(8,128)(2,1)S(1)} collective-permute-done((bf16[128,1024]{1,0:T(8,128)(2,1)S(1)}, bf16[128,1024]{1,0:T(8,128)(2,1)S(1)}, u32[]{:S(2)}, u32[]{:S(2)}) %collective-permute-start.6) | collective-permute-done | bytes 262176 | tf_op jit(solution)/shard_map/ppermute | solution.py:60
  44.9 0.0 collective-permute-done.4.other_ref
  44.9 1.5 shard_map.113
  46.4 3.0 %collective-permute-start.7 = (bf16[96,1024]{1,0:T(8,128)(2,1)S(1)}, bf16[96,1024]{1,0:T(8,128)(2,1)S(1)}, u32[]{:S(2)}, u32[]{:S(2)}) collective-permute-start(bf16[96,1024]{1,0:T(8,128)(2,1)S(1)} %get-tuple-element.27), channel_id=1, source_target_pairs={{0,2},{1,3},{2,0},{3,1},{4,6},{5,7},{6,4},{7,5},{8,10},{9,11},{10,... | collective-permute-start | bytes 589832 | tf_op jit(solution)/shard_map/ppermute | solution.py:60
  49.4 0.4 collective-permute-start.8
  49.8 2.3 collective-permute-start.9
  52.1 0.0 collective-permute-done.11.refs_0_
  52.1 1.5 shard_map.115
  53.6 0.1 collective-permute-start.12
  53.7 0.6 collective-permute-start.13
  54.3 4.7 %collective-permute-done.12.b = bf16[32,1024]{1,0:T(8,128)(2,1)S(1)} collective-permute-done((bf16[32,1024]{1,0:T(8,128)(2,1)S(1)}, bf16[32,1024]{1,0:T(8,128)(2,1)S(1)}, u32[]{:S(2)}, u32[]{:S(2)}) %collective-permute-start.12) | collective-permute-done | bytes 65568 | tf_op jit(solution)/shard_map/ppermute | solution.py:60
  59.0 2.3 %collective-permute-start.14 = (bf16[32,1024]{1,0:T(8,128)(2,1)S(1)}, bf16[32,1024]{1,0:T(8,128)(2,1)S(1)}, u32[]{:S(2)}, u32[]{:S(2)}) collective-permute-start(bf16[32,1024]{1,0:T(8,128)(2,1)S(1)} %get-tuple-element.35), channel_id=1, source_target_pairs={{0,3},{1,0},{2,1},{3,2},{4,7},{5,4},{6,5},{7,6},{8,11},{9,8},{10,9... | collective-permute-start | bytes 196616 | tf_op jit(solution)/shard_map/ppermute | solution.py:60
  61.3 0.0 collective-permute-done.13.c
  61.3 1.3 collective-permute-done.14.d
  62.7 0.1 collective-permute-start.15
  62.8 0.0 collective-permute-done.7.b
  62.8 0.0 collective-permute-done.8.c
  62.8 0.0 collective-permute-done.9.d
  62.8 0.1 shard_map.114
  62.9 1.2 collective-permute-start.10
  64.1 1.6 collective-permute-start.16
  65.7 1.8 collective-permute-done.15.p2
  67.5 0.5 collective-permute-done.10.p1
  68.0 0.0 collective-permute-done.16.p3
  68.0 0.0 copy-done.3
  68.0 0.0 copy-done.5
  68.0 0.2 shard_map.117
  68.3 4.5 %collective-permute-start.17 = (bf16[32,4096]{1,0:T(8,128)(2,1)S(1)}, bf16[32,4096]{1,0:T(8,128)(2,1)S(1)}, u32[]{:S(2)}, u32[]{:S(2)}) collective-permute-start(bf16[32,4096]{1,0:T(8,128)(2,1)S(1)} %get-tuple-element.37.own_ref), channel_id=1, source_target_pairs={{0,4},{4,0},{1,5},{5,1},{2,6},{6,2},{3,7},{7,3},{8,12},{12,8},{9,1... | collective-permute-start | bytes 786440 | tf_op jit(solution)/shard_map/ppermute | solution.py:60
  72.8 0.0 copy-done.6
  72.8 0.1 collective-permute-start
  72.9 1.1 collective-permute-done.sibling_ref
  74.1 0.5 shard_map.110
  74.6 0.0 collective-permute-done.17.other_ref
  74.6 1.3 shard_map.118
  75.9 2.0 copy-done
  77.8 8.2 %all-to-all-start = ((bf16[64,8,4096]{2,1,0:T(8,128)(2,1)}), bf16[64,8,4096]{2,1,0:T(8,128)(2,1)}, u32[]{:S(2)}, u32[]{:S(2)}) async-start(bf16[64,8,4096]{2,1,0:T(8,128)(2,1)} %bitcast.8), calls=%async_computation | async-start | bytes 8388608 | tf_op jit(solution)/shard_map/all_to_all | solution.py:289
  86.0 2.8 %shard_map.119.second_ref = bf16[2048,1536]{1,0:T(8,128)(2,1)S(1)} custom-call(bf16[1,4096,1536]{2,1,0:T(8,128)(2,1)} %source.1), custom_call_target="tpu_custom_call" | custom-call | flops 1000000000 | tf_op jit(solution)/shard_map/pallas_call | solution.py:43
  88.8 2.6 %copy-done.1 = bf16[2048,1536]{1,0:T(8,128)(2,1)} copy-done((bf16[2048,1536]{1,0:T(8,128)(2,1)}, bf16[2048,1536]{1,0:T(8,128)(2,1)S(1)}, u32[]{:S(2)}) %copy-start.1) | copy-done | bytes 6291480
  91.4 47.9 %all-to-all-done = bf16[64,8,4096]{2,1,0:T(8,128)(2,1)} async-done(((bf16[64,8,4096]{2,1,0:T(8,128)(2,1)}), bf16[64,8,4096]{2,1,0:T(8,128)(2,1)}, u32[]{:S(2)}, u32[]{:S(2)}) %all-to-all-start) | async-done | bytes 4194336 | tf_op jit(solution)/shard_map/all_to_all | solution.py:289
  139.4 2.8 %copy-done.2 = bf16[2048,1536]{1,0:T(8,128)(2,1)S(1)} copy-done((bf16[2048,1536]{1,0:T(8,128)(2,1)S(1)}, bf16[2048,1536]{1,0:T(8,128)(2,1)}, u32[]{:S(2)}) %copy-start.2) | copy-done | bytes 6291480
  142.2 2.8 %copy-done.8 = bf16[1,768,4096]{2,1,0:T(8,128)(2,1)S(1)} copy-done((bf16[1,768,4096]{2,1,0:T(8,128)(2,1)S(1)}, bf16[1,768,4096]{2,1,0:T(8,128)(2,1)}, u32[]{:S(2)}) %copy-start.8) | copy-done | bytes 6291480
  144.9 2.8 %copy-done.10 = bf16[2048,1536]{1,0:T(8,128)(2,1)S(1)} copy-done((bf16[2048,1536]{1,0:T(8,128)(2,1)S(1)}, bf16[2048,1536]{1,0:T(8,128)(2,1)}, u32[]{:S(2)}) %copy-start.10) | copy-done | bytes 6291480
  147.7 12.3 %shard_map.120 = bf16[512,4096]{1,0:T(8,128)(2,1)S(1)} custom-call(bf16[512,4096]{1,0:T(8,128)(2,1)} %bitcast.4.rows_ref, bf16[2048,1536]{1,0:T(8,128)(2,1)S(1)} %copy-done.10, bf16[2048,1536]{1,0:T(8,128)(2,1)S(1)} %copy-done.2, bf16[768,4096]{1,0:T(8,128)(2,1)S(1)} %bitcast.14), custom_call_target="tpu_custom_call" | custom-call | flops 10000000000 | tf_op jit(solution)/shard_map/pallas_call | solution.py:43
  160.0 62.1 %all_to_all.10 = bf16[64,8,4096]{2,1,0:T(8,128)(2,1)S(1)} all-to-all(bf16[64,8,4096]{2,1,0:T(8,128)(2,1)S(1)} %bitcast.10), channel_id=1, replica_groups=mesh['x'=4,'z'=4,'c'=2,'y'=4] {'x','z','y'}, dimensions={0} | all-to-all | bytes 8388608 | tf_op jit(solution)/shard_map/all_to_all | solution.py:297
  222.1 0.7 shard_map.121
  222.9 3.3 %collective-permute-start.18 = (f32[32,4096]{1,0:T(8,128)S(1)}, f32[32,4096]{1,0:T(8,128)S(1)}, u32[]{:S(2)}, u32[]{:S(2)}) collective-permute-start(f32[32,4096]{1,0:T(8,128)S(1)} %get-tuple-element.42), channel_id=1, source_target_pairs={{0,4},{4,0},{1,5},{5,1},{2,6},{6,2},{3,7},{7,3},{8,12},{12,8},{9,1... | collective-permute-start | bytes 1572872 | tf_op jit(solution)/shard_map/ppermute | solution.py:60
  226.2 1.5 collective-permute-done.18.other_ref
  227.7 0.7 shard_map.122
  (13 shorter events, 0.1 us)
Async XLA Ops:
  0.0 15.4 %collective-permute-start.1 = (bf16[1024,128]{1,0:T(8,128)(2,1)}, bf16[1024,128]{1,0:T(8,128)(2,1)S(1)}, u32[]{:S(2)}, u32[]{:S(2)}) collective-permute-start(bf16[1024,128]{1,0:T(8,128)(2,1)} %a.1), channel_id=1, source_target_pairs={{0,24},{8,0},{16,8},{24,16},{1,25},{9,1},{17,9},{25,17},{2,26},{10... | collective-permute-start | bytes 786440 | tf_op jit(solution)/shard_map/ppermute | solution.py:60
  4.6 10.8 %collective-permute-start.2 = (bf16[1024,128]{1,0:T(8,128)(2,1)}, bf16[1024,128]{1,0:T(8,128)(2,1)S(1)}, u32[]{:S(2)}, u32[]{:S(2)}) collective-permute-start(bf16[1024,128]{1,0:T(8,128)(2,1)} %a.1), channel_id=1, source_target_pairs={{0,16},{8,24},{16,0},{24,8},{1,17},{9,25},{17,1},{25,9},{2,18},{10... | collective-permute-start | bytes 786440 | tf_op jit(solution)/shard_map/ppermute | solution.py:60
  4.6 15.0 %collective-permute-start.3 = (bf16[1024,128]{1,0:T(8,128)(2,1)}, bf16[1024,128]{1,0:T(8,128)(2,1)S(1)}, u32[]{:S(2)}, u32[]{:S(2)}) collective-permute-start(bf16[1024,128]{1,0:T(8,128)(2,1)} %a.1), channel_id=1, source_target_pairs={{0,8},{8,16},{16,24},{24,0},{1,9},{9,17},{17,25},{25,1},{2,10},{10... | collective-permute-start | bytes 786440 | tf_op jit(solution)/shard_map/ppermute | solution.py:60
  19.6 1.0 copy-start.4
  20.7 24.2 %collective-permute-start.4 = (bf16[1024,512]{1,0:T(8,128)(2,1)S(1)}, bf16[1024,512]{1,0:T(8,128)(2,1)S(1)}, u32[]{:S(2)}, u32[]{:S(2)}) collective-permute-start(bf16[1024,512]{1,0:T(8,128)(2,1)S(1)} %shard_map.111.own_ref), channel_id=1, source_target_pairs={{0,4},{4,0},{1,5},{5,1},{2,6},{6,2},{3,7},{7,3},{8,12},{12,8},{9,1... | collective-permute-start | bytes 3145736 | tf_op jit(solution)/shard_map/ppermute | solution.py:60
  25.3 2.6 %copy-start.9 = (bf16[2048,1536]{1,0:T(8,128)(2,1)}, bf16[2048,1536]{1,0:T(8,128)(2,1)S(1)}, u32[]{:S(2)}) copy-start(bf16[2048,1536]{1,0:T(8,128)(2,1)S(1)} %get-tuple-element.38.first_ref) | copy-start | bytes 18874372
  27.9 40.1 %copy-start.3 = (bf16[32,4096]{1,0:T(8,128)(2,1)S(1)}, bf16[32,4096]{1,0:T(8,128)(2,1)}, u32[]{:S(2)}) copy-start(bf16[32,4096]{1,0:T(8,128)(2,1)} %residual_ref.1) | copy-start | bytes 786436
  27.9 40.1 %copy-start.5 = (f32[4096]{0:T(1024)S(1)}, f32[4096]{0:T(1024)}, u32[]{:S(2)}) copy-start(f32[4096]{0:T(1024)} %param.17) | copy-start | bytes 49156
  27.9 44.9 %copy-start.6 = (s32[32,8]{0,1:T(8,128)S(1)}, s32[32,8]{0,1:T(8,128)}, u32[]{:S(2)}) copy-start(s32[32,8]{0,1:T(8,128)} %param.18) | copy-start | bytes 3076
  27.9 44.9 %copy-start.7 = (f32[32,8]{0,1:T(8,128)S(1)}, f32[32,8]{0,1:T(8,128)}, u32[]{:S(2)}) copy-start(f32[32,8]{0,1:T(8,128)} %param.19) | copy-start | bytes 3076
  27.9 13.7 %collective-permute-start.5 = (bf16[128,1024]{1,0:T(8,128)(2,1)S(1)}, bf16[128,1024]{1,0:T(8,128)(2,1)S(1)}, u32[]{:S(2)}, u32[]{:S(2)}) collective-permute-start(bf16[128,1024]{1,0:T(8,128)(2,1)S(1)} %get-tuple-element.25.refs_0_), channel_id=1, source_target_pairs={{0,96},{32,0},{64,32},{96,64},{1,97},{33,1},{65,33},{97,65},{2,98}... | collective-permute-start | bytes 786440 | tf_op jit(solution)/shard_map/ppermute | solution.py:60
  30.5 14.4 %collective-permute-start.6 = (bf16[128,1024]{1,0:T(8,128)(2,1)S(1)}, bf16[128,1024]{1,0:T(8,128)(2,1)S(1)}, u32[]{:S(2)}, u32[]{:S(2)}) collective-permute-start(bf16[128,1024]{1,0:T(8,128)(2,1)S(1)} %get-tuple-element.25.refs_0_), channel_id=1, source_target_pairs={{0,32},{32,64},{64,96},{96,0},{1,33},{33,65},{65,97},{97,1},{2,34}... | collective-permute-start | bytes 786440 | tf_op jit(solution)/shard_map/ppermute | solution.py:60
  30.5 21.6 %collective-permute-start.11 = (bf16[128,1024]{1,0:T(8,128)(2,1)S(1)}, bf16[128,1024]{1,0:T(8,128)(2,1)S(1)}, u32[]{:S(2)}, u32[]{:S(2)}) collective-permute-start(bf16[128,1024]{1,0:T(8,128)(2,1)S(1)} %get-tuple-element.25.refs_0_), channel_id=1, source_target_pairs={{0,64},{32,96},{64,0},{96,32},{1,65},{33,97},{65,1},{97,33},{2,66}... | collective-permute-start | bytes 786440 | tf_op jit(solution)/shard_map/ppermute | solution.py:60
  46.4 16.4 %collective-permute-start.7 = (bf16[96,1024]{1,0:T(8,128)(2,1)S(1)}, bf16[96,1024]{1,0:T(8,128)(2,1)S(1)}, u32[]{:S(2)}, u32[]{:S(2)}) collective-permute-start(bf16[96,1024]{1,0:T(8,128)(2,1)S(1)} %get-tuple-element.27), channel_id=1, source_target_pairs={{0,2},{1,3},{2,0},{3,1},{4,6},{5,7},{6,4},{7,5},{8,10},{9,11},{10,... | collective-permute-start | bytes 589832 | tf_op jit(solution)/shard_map/ppermute | solution.py:60
  49.4 13.4 %collective-permute-start.8 = (bf16[96,1024]{1,0:T(8,128)(2,1)S(1)}, bf16[96,1024]{1,0:T(8,128)(2,1)S(1)}, u32[]{:S(2)}, u32[]{:S(2)}) collective-permute-start(bf16[96,1024]{1,0:T(8,128)(2,1)S(1)} %get-tuple-element.28), channel_id=1, source_target_pairs={{0,1},{1,2},{2,3},{3,0},{4,5},{5,6},{6,7},{7,4},{8,9},{9,10},{10,1... | collective-permute-start | bytes 589832 | tf_op jit(solution)/shard_map/ppermute | solution.py:60
  49.8 13.0 %collective-permute-start.9 = (bf16[96,1024]{1,0:T(8,128)(2,1)S(1)}, bf16[96,1024]{1,0:T(8,128)(2,1)S(1)}, u32[]{:S(2)}, u32[]{:S(2)}) collective-permute-start(bf16[96,1024]{1,0:T(8,128)(2,1)S(1)} %get-tuple-element.29), channel_id=1, source_target_pairs={{0,3},{1,0},{2,1},{3,2},{4,7},{5,4},{6,5},{7,6},{8,11},{9,8},{10,9... | collective-permute-start | bytes 589832 | tf_op jit(solution)/shard_map/ppermute | solution.py:60
  53.6 5.4 %collective-permute-start.12 = (bf16[32,1024]{1,0:T(8,128)(2,1)S(1)}, bf16[32,1024]{1,0:T(8,128)(2,1)S(1)}, u32[]{:S(2)}, u32[]{:S(2)}) collective-permute-start(bf16[32,1024]{1,0:T(8,128)(2,1)S(1)} %get-tuple-element.33), channel_id=1, source_target_pairs={{0,2},{1,3},{2,0},{3,1},{4,6},{5,7},{6,4},{7,5},{8,10},{9,11},{10,... | collective-permute-start | bytes 196616 | tf_op jit(solution)/shard_map/ppermute | solution.py:60
  53.7 7.6 %collective-permute-start.13 = (bf16[32,1024]{1,0:T(8,128)(2,1)S(1)}, bf16[32,1024]{1,0:T(8,128)(2,1)S(1)}, u32[]{:S(2)}, u32[]{:S(2)}) collective-permute-start(bf16[32,1024]{1,0:T(8,128)(2,1)S(1)} %get-tuple-element.34), channel_id=1, source_target_pairs={{0,1},{1,2},{2,3},{3,0},{4,5},{5,6},{6,7},{7,4},{8,9},{9,10},{10,1... | collective-permute-start | bytes 196616 | tf_op jit(solution)/shard_map/ppermute | solution.py:60
  59.0 3.7 %collective-permute-start.14 = (bf16[32,1024]{1,0:T(8,128)(2,1)S(1)}, bf16[32,1024]{1,0:T(8,128)(2,1)S(1)}, u32[]{:S(2)}, u32[]{:S(2)}) collective-permute-start(bf16[32,1024]{1,0:T(8,128)(2,1)S(1)} %get-tuple-element.35), channel_id=1, source_target_pairs={{0,3},{1,0},{2,1},{3,2},{4,7},{5,4},{6,5},{7,6},{8,11},{9,8},{10,9... | collective-permute-start | bytes 196616 | tf_op jit(solution)/shard_map/ppermute | solution.py:60
  62.7 4.8 %collective-permute-start.15 = (bf16[32,1024]{1,0:T(8,128)(2,1)S(1)}, bf16[32,1024]{1,0:T(8,128)(2,1)S(1)}, u32[]{:S(2)}, u32[]{:S(2)}) collective-permute-start(bf16[32,1024]{1,0:T(8,128)(2,1)S(1)} %shard_map.116), channel_id=1, source_target_pairs={{0,64},{32,96},{64,0},{96,32},{1,65},{33,97},{65,1},{97,33},{2,66}... | collective-permute-start | bytes 196616 | tf_op jit(solution)/shard_map/ppermute | solution.py:60
  62.9 5.1 %collective-permute-start.10 = (bf16[32,1024]{1,0:T(8,128)(2,1)S(1)}, bf16[32,1024]{1,0:T(8,128)(2,1)S(1)}, u32[]{:S(2)}, u32[]{:S(2)}) collective-permute-start(bf16[32,1024]{1,0:T(8,128)(2,1)S(1)} %get-tuple-element.31), channel_id=1, source_target_pairs={{0,32},{32,64},{64,96},{96,0},{1,33},{33,65},{65,97},{97,1},{2,34}... | collective-permute-start | bytes 196616 | tf_op jit(solution)/shard_map/ppermute | solution.py:60
  64.1 3.9 %collective-permute-start.16 = (bf16[32,1024]{1,0:T(8,128)(2,1)S(1)}, bf16[32,1024]{1,0:T(8,128)(2,1)S(1)}, u32[]{:S(2)}, u32[]{:S(2)}) collective-permute-start(bf16[32,1024]{1,0:T(8,128)(2,1)S(1)} %get-tuple-element.36), channel_id=1, source_target_pairs={{0,96},{32,0},{64,32},{96,64},{1,97},{33,1},{65,33},{97,65},{2,98}... | collective-permute-start | bytes 196616 | tf_op jit(solution)/shard_map/ppermute | solution.py:60
  68.3 6.3 %collective-permute-start.17 = (bf16[32,4096]{1,0:T(8,128)(2,1)S(1)}, bf16[32,4096]{1,0:T(8,128)(2,1)S(1)}, u32[]{:S(2)}, u32[]{:S(2)}) collective-permute-start(bf16[32,4096]{1,0:T(8,128)(2,1)S(1)} %get-tuple-element.37.own_ref), channel_id=1, source_target_pairs={{0,4},{4,0},{1,5},{5,1},{2,6},{6,2},{3,7},{7,3},{8,12},{12,8},{9,1... | collective-permute-start | bytes 786440 | tf_op jit(solution)/shard_map/ppermute | solution.py:60
  72.8 1.3 collective-permute-start
  75.9 2.0 copy-start
  77.8 61.5 %all-to-all-start = ((bf16[64,8,4096]{2,1,0:T(8,128)(2,1)}), bf16[64,8,4096]{2,1,0:T(8,128)(2,1)}, u32[]{:S(2)}, u32[]{:S(2)}) async-start(bf16[64,8,4096]{2,1,0:T(8,128)(2,1)} %bitcast.8), calls=%async_computation | async-start | bytes 8388608 | tf_op jit(solution)/shard_map/all_to_all | solution.py:289
  88.8 2.6 %copy-start.1 = (bf16[2048,1536]{1,0:T(8,128)(2,1)}, bf16[2048,1536]{1,0:T(8,128)(2,1)S(1)}, u32[]{:S(2)}) copy-start(bf16[2048,1536]{1,0:T(8,128)(2,1)S(1)} %shard_map.119.second_ref) | copy-start | bytes 18874372
  139.4 2.8 %copy-start.2 = (bf16[2048,1536]{1,0:T(8,128)(2,1)S(1)}, bf16[2048,1536]{1,0:T(8,128)(2,1)}, u32[]{:S(2)}) copy-start(bf16[2048,1536]{1,0:T(8,128)(2,1)} %copy-done.1) | copy-start | bytes 18874372
  142.2 2.8 %copy-start.8 = (bf16[1,768,4096]{2,1,0:T(8,128)(2,1)S(1)}, bf16[1,768,4096]{2,1,0:T(8,128)(2,1)}, u32[]{:S(2)}) copy-start(bf16[1,768,4096]{2,1,0:T(8,128)(2,1)} %param.21) | copy-start | bytes 18874372
  144.9 2.8 %copy-start.10 = (bf16[2048,1536]{1,0:T(8,128)(2,1)S(1)}, bf16[2048,1536]{1,0:T(8,128)(2,1)}, u32[]{:S(2)}) copy-start(bf16[2048,1536]{1,0:T(8,128)(2,1)} %copy-done.9) | copy-start | bytes 18874372
  222.9 4.9 %collective-permute-start.18 = (f32[32,4096]{1,0:T(8,128)S(1)}, f32[32,4096]{1,0:T(8,128)S(1)}, u32[]{:S(2)}, u32[]{:S(2)}) collective-permute-start(f32[32,4096]{1,0:T(8,128)S(1)} %get-tuple-element.42), channel_id=1, source_target_pairs={{0,4},{4,0},{1,5},{5,1},{2,6},{6,2},{3,7},{7,3},{8,12},{12,8},{9,1... | collective-permute-start | bytes 1572872 | tf_op jit(solution)/shard_map/ppermute | solution.py:60
